TPU v7x, 32 devices: a whole 2x2x4 slice. The times are simulated.
32 devices in a mesh: dp: 8 (over z, x), mp: 4 (over y, core).
Axes of the slice: x: 2, y: 2, z: 4, core: 2. Of those that a mesh axis runs over, the one named last changes fastest.
Arguments:
- text_in: bfloat16 [7680, 768], P(('dp', 'mp')), may hold values from -6 to 6
- caption_ids: int32 [480, 16], P('dp'), may hold values from 0 to 31999, as said below
- pairing: int32 [480], replicated, may hold values from 0 to 479, each once
- image_low: bfloat16 [19200, 768], P(('dp', 'mp')), may hold values from -6 to 6
- image_high: bfloat16 [13920, 768], P(('dp', 'mp')), may hold values from -6 to 6
- img_gains: float32 [2, 768], replicated, may hold values from 0.5 to 1.5
- img_qkv: bfloat16 [3, 768, 768], P(None, None, 'mp'), may hold values from -0.21875 to 0.21875
- img_out: bfloat16 [768, 768], P('mp'), may hold values from -0.625 to 0.625
- img_fc1: bfloat16 [768, 3072], P(None, 'mp'), may hold values from -0.21875 to 0.21875
- img_fc2: bfloat16 [3072, 768], P('mp'), may hold values from -0.109375 to 0.109375
- txt_qkv: bfloat16 [3, 768, 768], P(None, None, 'mp'), may hold values from -0.21875 to 0.21875
- txt_qv_bias: float32 [2, 768], P(None, 'mp'), may hold values from -3 to 3
- txt_out: bfloat16 [768, 768], P('mp'), may hold values from -0.4375 to 0.4375
- txt_fc1: bfloat16 [768, 3072], P(None, 'mp'), may hold values from -0.21875 to 0.21875
- txt_fc1_bias: float32 [3072], P('mp'), may hold values from -3 to 3
- txt_fc2: bfloat16 [3072, 768], P('mp'), may hold values from -0.109375 to 0.109375
- txt_gains: float32 [2, 768], replicated, may hold values from 0.5 to 1.5
- txt_shifts: float32 [2, 768], replicated, may hold values from -2 to 2
- txt_biases: float32 [2, 768], replicated, may hold values from -2 to 2
Outputs:
- loss: float32 [], replicated
- grad_text_in: float32 [7680, 768], P(('dp', 'mp'))
- grad_qkv: float32 [3, 768, 768], P(None, None, 'mp')
- grad_qv_bias: float32 [2, 768], P(None, 'mp')
- grad_out: float32 [768, 768], P('mp')
- grad_fc1: float32 [768, 3072], P(None, 'mp')
- grad_fc1_bias: float32 [3072], P('mp')
- grad_fc2: float32 [3072, 768], P('mp')
- grad_gains: float32 [2, 768], replicated
- grad_shifts: float32 [2, 768], replicated
- grad_biases: float32 [2, 768], replicated
Inputs may be any that keep to these rules, and one draw needn't show every extreme that they name: `caption_ids`: in each caption the nonzero ids come first and the zeros after; each caption has 4 to 16 nonzero ids. Image i is paired with caption pairing[i]; each caption is paired once.
All inputs are finite; a program needn't handle non-finite values.
Results may differ from a plain program's by a relative error of at most 0.017.
Values may be sent and summed in bfloat16 or wider, within the bound.
A program may use at most 192 MiB of HBM per device.

v0:
```python
import jax
import jax.numpy as jnp
from jax import lax
from jax.sharding import PartitionSpec as P

D = 768
HEAD = 64
L = 16
P_LOW = 50
P_HIGH = 145
EPS = 1e-06
SCALE = 40.0
LOSS_SCALE = 16.0
MASKED = -1e30


def layer_stats(values):
    center = values - jnp.mean(values, -1, keepdims=True)
    inverse = lax.rsqrt(jnp.mean(center * center, -1, keepdims=True) + EPS)
    return (center * inverse, inverse)


def norm_back(grad_out, unit, inverse, gain):
    scaled = grad_out * gain
    return inverse * (
        scaled
        - jnp.mean(scaled, -1, keepdims=True)
        - unit * jnp.mean(scaled * unit, -1, keepdims=True)
    )


def gelu_exact(values):
    return jax.nn.gelu(values, approximate=False)


def score_rows(queries, keys_all, keep):
    scores = (
        jnp.einsum("nqhe,nkhe->nhqk", queries, keys_all, preferred_element_type=jnp.float32) * 0.125
    )
    if keep is not None:
        scores = jnp.where(keep, scores, MASKED)
    return scores


def attention_shares(queries, keys_all, keep):
    scores = score_rows(queries, keys_all, keep)
    highest = jnp.max(scores, -1, keepdims=True)
    raised = jnp.exp(scores - highest)
    totals = jnp.sum(raised, -1, keepdims=True)
    return (raised / totals, highest + jnp.log(totals))


def image_tower(tokens, count, length, gains, weights):
    w_qkv, w_out, w_fc1, w_fc2 = weights
    head_count = D // HEAD
    inputs = tokens.astype(jnp.float32)
    unit, spare = layer_stats(inputs)
    normed = (unit * gains[0]).astype(jnp.bfloat16)
    projected = jnp.einsum("rd,jdw->jrw", normed, w_qkv, preferred_element_type=jnp.float32).astype(
        jnp.bfloat16
    )
    shaped = projected.reshape(3, count, length, head_count, HEAD)
    shares, spare_lse = attention_shares(shaped[0], shaped[1], None)
    context = jnp.einsum(
        "nhqk,nkhe->nqhe",
        shares.astype(jnp.bfloat16),
        shaped[2],
        preferred_element_type=jnp.float32,
    )
    context = context.astype(jnp.bfloat16).reshape(count * length, D)
    middle = inputs + jnp.dot(context, w_out, preferred_element_type=jnp.float32)
    unit2, spare2 = layer_stats(middle)
    normed2 = (unit2 * gains[1]).astype(jnp.bfloat16)
    active = gelu_exact(jnp.dot(normed2, w_fc1, preferred_element_type=jnp.float32)).astype(
        jnp.bfloat16
    )
    result = middle + jnp.dot(active, w_fc2, preferred_element_type=jnp.float32)
    pooled = jnp.mean(result.reshape(count, length, D), 1)
    return (pooled * lax.rsqrt(jnp.sum(pooled * pooled, -1, keepdims=True) + EPS)).astype(
        jnp.bfloat16
    )


def local(
    text_in,
    caption_ids,
    pairing,
    image_low,
    image_high,
    img_gains,
    img_qkv,
    img_out,
    img_fc1,
    img_fc2,
    txt_qkv,
    txt_qv_bias,
    txt_out,
    txt_fc1,
    txt_fc1_bias,
    txt_fc2,
    txt_gains,
    txt_shifts,
    txt_biases,
):
    weights = (
        lax.all_gather(img_qkv, "mp", axis=2, tiled=True),
        lax.all_gather(img_out, "mp", axis=0, tiled=True),
        lax.all_gather(img_fc1, "mp", axis=1, tiled=True),
        lax.all_gather(img_fc2, "mp", axis=0, tiled=True),
    )
    low_count = image_low.shape[0] // P_LOW
    high_count = image_high.shape[0] // P_HIGH
    images16 = jnp.concatenate(
        [
            image_tower(image_low, low_count, P_LOW, img_gains, weights),
            image_tower(image_high, high_count, P_HIGH, img_gains, weights),
        ],
        0,
    )
    width = txt_qkv.shape[2]
    head_count = width // HEAD
    own_rows = text_in.shape[0]
    own_caps = own_rows // L
    group_caps = caption_ids.shape[0]
    group_rows = group_caps * L
    own_ids = lax.dynamic_slice_in_dim(caption_ids, lax.axis_index("mp") * own_caps, own_caps, 0)
    keep = (caption_ids > 0)[:, None, None, :]
    inputs = text_in.astype(jnp.float32)
    unit1, inverse1 = layer_stats(inputs)
    normed1 = (unit1 * txt_gains[0] + txt_shifts[0]).astype(jnp.bfloat16)
    bias_rows = jnp.stack([txt_qv_bias[0], jnp.zeros_like(txt_qv_bias[0]), txt_qv_bias[1]])
    piece = lax.all_gather(normed1, "mp", axis=0, tiled=True)
    made = jnp.einsum("rd,jdw->rjw", piece, txt_qkv, preferred_element_type=jnp.float32) + bias_rows
    joined = jnp.concatenate(
        [piece, made.astype(jnp.bfloat16).reshape(piece.shape[0], 3 * width)], 1
    )
    normed1_all = joined[:, :D]
    triple = joined[:, D:].reshape(group_caps, L, 3, head_count, HEAD)
    queries = triple[:, :, 0]
    keys_all = triple[:, :, 1]
    values_all = triple[:, :, 2]
    shares, log_totals = attention_shares(queries, keys_all, keep)
    context = jnp.einsum(
        "nhqk,nkhe->nqhe",
        shares.astype(jnp.bfloat16),
        values_all,
        preferred_element_type=jnp.float32,
    )
    context = context.astype(jnp.bfloat16).reshape(group_rows, width)
    middle = inputs + (
        lax.psum_scatter(
            jnp.dot(context, txt_out, preferred_element_type=jnp.float32).astype(jnp.bfloat16),
            "mp",
            scatter_dimension=0,
            tiled=True,
        ).astype(jnp.float32)
        + txt_biases[0]
    )
    unit2, inverse2 = layer_stats(middle)
    normed2 = (unit2 * txt_gains[1] + txt_shifts[1]).astype(jnp.bfloat16)
    piece = lax.all_gather(normed2, "mp", axis=0, tiled=True)
    hidden_piece = jnp.dot(piece, txt_fc1, preferred_element_type=jnp.float32) + txt_fc1_bias
    spread = jnp.concatenate([piece.astype(jnp.float32), hidden_piece], 1)
    normed2_all = spread[:, :D].astype(jnp.bfloat16)
    hidden = spread[:, D:]
    active, gelu_pull = jax.vjp(gelu_exact, hidden)
    active16 = active.astype(jnp.bfloat16)
    result = middle + (
        lax.psum_scatter(
            jnp.dot(active16, txt_fc2, preferred_element_type=jnp.float32).astype(jnp.bfloat16),
            "mp",
            scatter_dimension=0,
            tiled=True,
        ).astype(jnp.float32)
        + txt_biases[1]
    )
    present = (own_ids > 0).astype(jnp.float32)
    counts = jnp.sum(present, 1, keepdims=True)
    pooled = jnp.sum(result.reshape(own_caps, L, D) * present[:, :, None], 1) / counts
    inverse_len = lax.rsqrt(jnp.sum(pooled * pooled, -1, keepdims=True) + EPS)
    captions_unit = pooled * inverse_len
    captions16 = captions_unit.astype(jnp.bfloat16)
    total_pairs = pairing.shape[0]
    first_pair = lax.axis_index(("dp", "mp")) * own_caps
    arrived = lax.all_gather(captions16, ("dp", "mp"), axis=0, tiled=True)
    logits = SCALE * jnp.einsum("id,jd->ij", images16, arrived, preferred_element_type=jnp.float32)
    targets = lax.dynamic_slice_in_dim(pairing, first_pair, own_caps, 0)
    matched = (targets[:, None] == jnp.arange(total_pairs)[None, :]).astype(jnp.float32)
    raised = jnp.exp(logits - SCALE)
    local_lse = SCALE + jnp.log(jnp.sum(raised, 1))
    partial_value = jnp.sum(raised, 0)
    own_term = 0.5 * jnp.sum(local_lse) - jnp.sum(matched * logits)
    summed, scalar = lax.psum((partial_value, own_term), ("dp", "mp"))
    other_lse = SCALE + jnp.log(summed)
    total = scalar + 0.5 * jnp.sum(other_lse)
    loss = total / total_pairs
    grads16 = (
        LOSS_SCALE
        * (
            0.5 * jnp.exp(logits - local_lse[:, None])
            + 0.5 * jnp.exp(logits - other_lse[None, :])
            - matched
        )
    ).astype(jnp.bfloat16)
    grad_caps = lax.psum_scatter(
        SCALE * jnp.einsum("ic,id->cd", grads16, images16, preferred_element_type=jnp.float32),
        ("dp", "mp"),
        scatter_dimension=0,
        tiled=True,
    )
    grad_pooled = inverse_len * (
        grad_caps - captions_unit * jnp.sum(captions_unit * grad_caps, -1, keepdims=True)
    )
    grad_result = (grad_pooled[:, None, :] * (present / counts)[:, :, None]).reshape(own_rows, D)
    grad_all = lax.all_gather(grad_result.astype(jnp.bfloat16), "mp", axis=0, tiled=True)
    grad_fc2 = jnp.einsum("gf,gd->fd", active16, grad_all, preferred_element_type=jnp.float32)
    grad_active = jnp.einsum("gd,fd->gf", grad_all, txt_fc2, preferred_element_type=jnp.float32)
    grad_hidden16 = gelu_pull(grad_active)[0].astype(jnp.bfloat16)
    grad_fc1 = jnp.einsum(
        "gd,gf->df", normed2_all, grad_hidden16, preferred_element_type=jnp.float32
    )
    grad_fc1_bias = jnp.sum(grad_hidden16.astype(jnp.float32), 0)
    grad_normed2 = lax.psum_scatter(
        jnp.einsum("gf,df->gd", grad_hidden16, txt_fc1, preferred_element_type=jnp.float32).astype(
            jnp.bfloat16
        ),
        "mp",
        scatter_dimension=0,
        tiled=True,
    ).astype(jnp.float32)
    grad_middle = grad_result + norm_back(grad_normed2, unit2, inverse2, txt_gains[1])
    grad_mid_all = lax.all_gather(grad_middle.astype(jnp.bfloat16), "mp", axis=0, tiled=True)
    grad_out = jnp.einsum("gw,gd->wd", context, grad_mid_all, preferred_element_type=jnp.float32)
    grad_context = jnp.einsum(
        "gd,wd->gw", grad_mid_all, txt_out, preferred_element_type=jnp.float32
    )
    grad_context = grad_context.astype(jnp.bfloat16).reshape(group_caps, L, head_count, HEAD)
    shares_again = jnp.exp(score_rows(queries, keys_all, keep) - log_totals)
    grad_shares = jnp.einsum(
        "nqhe,nkhe->nhqk", grad_context, values_all, preferred_element_type=jnp.float32
    )
    grad_values = jnp.einsum(
        "nhqk,nqhe->nkhe",
        shares_again.astype(jnp.bfloat16),
        grad_context,
        preferred_element_type=jnp.float32,
    ).astype(jnp.bfloat16)
    grad_scores = (
        shares_again * (grad_shares - jnp.sum(grad_shares * shares_again, -1, keepdims=True))
    ).astype(jnp.bfloat16)
    grad_queries = (
        jnp.einsum("nhqk,nkhe->nqhe", grad_scores, keys_all, preferred_element_type=jnp.float32)
        * 0.125
    ).astype(jnp.bfloat16)
    grad_keys = (
        jnp.einsum("nhqk,nqhe->nkhe", grad_scores, queries, preferred_element_type=jnp.float32)
        * 0.125
    ).astype(jnp.bfloat16)
    grad_triple = jnp.stack([grad_queries, grad_keys, grad_values], 0).reshape(3, group_rows, width)
    grad_qkv = jnp.einsum(
        "gd,jgw->jdw", normed1_all, grad_triple, preferred_element_type=jnp.float32
    )
    grad_qv_bias = jnp.stack(
        [
            jnp.sum(grad_triple[0].astype(jnp.float32), 0),
            jnp.sum(grad_triple[2].astype(jnp.float32), 0),
        ]
    )
    grad_normed1 = lax.psum_scatter(
        jnp.einsum("jgw,jdw->gd", grad_triple, txt_qkv, preferred_element_type=jnp.float32).astype(
            jnp.bfloat16
        ),
        "mp",
        scatter_dimension=0,
        tiled=True,
    ).astype(jnp.float32)
    grad_inputs = grad_middle + norm_back(grad_normed1, unit1, inverse1, txt_gains[0])
    summed_grads = lax.psum(
        (grad_qkv, grad_qv_bias, grad_out, grad_fc1, grad_fc1_bias, grad_fc2), "dp"
    )
    small_parts = jnp.stack(
        [
            jnp.sum(grad_normed1 * unit1, 0),
            jnp.sum(grad_normed2 * unit2, 0),
            jnp.sum(grad_normed1, 0),
            jnp.sum(grad_normed2, 0),
            jnp.sum(grad_middle, 0),
            jnp.sum(grad_result, 0),
        ]
    )
    shared = lax.psum(small_parts, ("dp", "mp"))
    return (
        loss,
        grad_inputs,
        summed_grads[0],
        summed_grads[1],
        summed_grads[2],
        summed_grads[3],
        summed_grads[4],
        summed_grads[5],
        shared[0:2],
        shared[2:4],
        shared[4:6],
    )


def solution(mesh):
    placed = (
        P(("dp", "mp"), None),
        P("dp", None),
        P(),
        P(("dp", "mp"), None),
        P(("dp", "mp"), None),
        P(),
        P(None, None, "mp"),
        P("mp", None),
        P(None, "mp"),
        P("mp", None),
        P(None, None, "mp"),
        P(None, "mp"),
        P("mp", None),
        P(None, "mp"),
        P("mp"),
        P("mp", None),
        P(),
        P(),
        P(),
    )
    return jax.shard_map(
        local,
        mesh=mesh,
        in_specs=placed,
        out_specs=(
            P(),
            P(("dp", "mp"), None),
            P(None, None, "mp"),
            P(None, "mp"),
            P("mp", None),
            P(None, "mp"),
            P("mp"),
            P("mp", None),
            P(),
            P(),
            P(),
        ),
        check_vma=False,
    )
```

profile of v0, /device:TPU:0, one launch (start us, length us, event | category | flops | bytes accessed | tf_op | source)
XLA Modules:
  0.0 829.3 jit_solution(6300139161258848959)
XLA Ops:
  14.9 20.2 %all-gather.18.cloned.1.call-done = bf16[960,768]{1,0:T(8,128)(2,1)} async-done(((bf16[240,768]{1,0:T(8,128)(2,1)}), bf16[960,768]{1,0:T(8,128)(2,1)}) %all-gather.18.cloned.1.call-update) | async-done | bytes 1474576 | tf_op jit(solution)/shard_map/all_gather | solution.py:132
  40.9 3.0 reshape_reshape.3
  43.9 3.2 fusion.221
  59.0 20.6 %reduce-scatter.7.cloned.1.call-done = bf16[240,768]{1,0:T(8,128)(2,1)} async-done(((bf16[960,768]{1,0:T(8,128)(2,1)}), bf16[240,768]{1,0:T(8,128)(2,1)}) %reduce-scatter.7.cloned.1.call-update) | async-done | bytes 368656 | tf_op jit(solution)/shard_map/reduce_scatter | solution.py:151
  84.2 27.8 %all-gather.10.cloned.1.call-done = bf16[3,768,768]{1,2,0:T(8,128)(2,1)} async-done(((bf16[3,768,192]{1,2,0:T(8,128)(2,1)}), bf16[3,768,768]{1,2,0:T(8,128)(2,1)}) %all-gather.10.cloned.1.call-update) | async-done | bytes 3538960 | tf_op jit(solution)/shard_map/all_gather | solution.py:106
  112.0 4.5 convert_bitcast_fusion
  117.9 4.5 squeeze.30
  122.4 4.1 squeeze.31
  126.5 3.8 fusion.45
  130.3 3.2 fusion.229
  136.3 4.5 convert_bitcast_fusion.1
  142.7 4.2 reshape.220
  156.6 3.3 reshape.237
  162.3 3.8 fusion.227
  168.5 4.1 fusion.69
  179.6 29.0 %all-gather.16.cloned.1.call-done = bf16[3072,768]{1,0:T(8,128)(2,1)} async-done(((bf16[768,768]{1,0:T(8,128)(2,1)}), bf16[3072,768]{1,0:T(8,128)(2,1)}) %all-gather.16.cloned.1.call-update) | async-done | bytes 4718608 | tf_op jit(solution)/shard_map/all_gather | solution.py:109
  208.6 25.3 %fusion.58 = f32[600,768]{1,0:T(8,128)S(1)} fusion(f32[600,768]{1,0:T(8,128)} %copy-done.23, bf16[3072,768]{1,0:T(8,128)(2,1)} %all-gather.16.cloned.1.call-done, bf16[768,3072]{1,0:T(8,128)(2,1)} %all-gather.14.cloned.1.call-done, f32[768]{0:T(1024)S(1)} %get-tuple-element.22, f32[600]{0:T(1024)S(1)} %add_rsqrt_fusion, f32[600]{0:T(1024)S(1)} %broadcast_multiply_fusion), kind=kOutput, calls=%fused_computation.102 | convolution fusion | flops 5784422400 | bytes 13131456 | tf_op jit(solution)/shard_map/dot_general | solution.py:77
  234.0 10.1 %multiply_convert_fusion = (bf16[960,768]{1,0:T(8,128)(2,1)S(1)}, f32[960,768]{1,0:T(8,128)}, f32[960,768]{1,0:T(8,128)}) fusion(f32[768]{0:T(1024)S(1)} %copy-done.64, bf16[960,768]{1,0:T(8,128)(2,1)} %all-gather.20.cloned.1.call-done, bf16[768,768]{1,0:T(8,128)(2,1)S(1)} %copy-done), kind=kOutput, calls=%fused_computation.54 | convolution fusion | flops 1181122560 | bytes 10030080 | tf_op jit(solution)/shard_map/dot_general | solution.py:162
  248.0 20.6 %fusion.62 = f32[435,768]{1,0:T(8,128)} fusion(f32[435,768]{1,0:T(8,128)} %copy-done.25, bf16[3072,768]{1,0:T(8,128)(2,1)} %all-gather.16.cloned.1.call-done, bf16[768,3072]{1,0:T(8,128)(2,1)} %all-gather.14.cloned.1.call-done, f32[768]{0:T(1024)S(1)} %get-tuple-element.22, f32[435]{0:T(512)S(1)} %add_rsqrt_fusion.2, f32[435]{0:T(512)S(1)} %broadcast_multiply_fusion.2), kind=kOutput, calls=%fused_computation.115 | convolution fusion | flops 4193706240 | bytes 12116376 | tf_op jit(solution)/shard_map/dot_general | solution.py:77
  277.0 42.7 %all-gather = bf16[32,15,768]{2,1,0:T(8,128)(2,1)S(1)} all-gather(bf16[1,15,768]{2,1,0:T(8,128)(2,1)S(1)} %fusion.139), channel_id=1, replica_groups=mesh['dp'=8,'mp'=4] {'dp','mp'}, dimensions={0}, use_global_device_ids=true | all-gather | bytes 760320 | tf_op jit(solution)/shard_map/all_gather | solution.py:185
  321.5 36.8 %psum.64 = f32[480]{0:T(512)S(1)} all-reduce(f32[480]{0:T(512)S(1)} %get-tuple-element.19), channel_id=1, replica_groups=mesh['dp'=8,'mp'=4] {'dp','mp'}, use_global_device_ids=true, to_apply=%region_32.33 | all-reduce | flops 480 | bytes 3840 | tf_op jit(solution)/shard_map/psum | solution.py:193
  360.7 77.1 %fusion = f32[16,768]{1,0:T(8,128)S(1)} fusion(f32[480,768]{1,0:T(8,128)S(1)} %convolution_multiply_fusion), kind=kCustom, calls=%all-reduce-scatter | all-reduce-scatter fusion | flops 393217 | bytes 1523712
  445.0 18.3 %all-gather.22.cloned.1.call-done = bf16[960,768]{1,0:T(8,128)(2,1)} async-done(((bf16[240,768]{1,0:T(8,128)(2,1)}), bf16[960,768]{1,0:T(8,128)(2,1)}) %all-gather.22.cloned.1.call-update) | async-done | bytes 1474576 | tf_op jit(solution)/shard_map/all_gather | solution.py:215
  463.3 5.6 convert_reduce_fusion
  472.6 27.5 %reduce-scatter.11.cloned.1.call-done = bf16[240,768]{1,0:T(8,128)(2,1)} async-done(((bf16[960,768]{1,0:T(8,128)(2,1)}), bf16[240,768]{1,0:T(8,128)(2,1)}) %reduce-scatter.11.cloned.1.call-update) | async-done | bytes 368656 | tf_op jit(solution)/shard_map/reduce_scatter | solution.py:223
  505.8 18.1 %all-gather.24.cloned.1.call-done = bf16[960,768]{1,0:T(8,128)(2,1)} async-done(((bf16[240,768]{1,0:T(8,128)(2,1)}), bf16[960,768]{1,0:T(8,128)(2,1)}) %all-gather.24.cloned.1.call-update) | async-done | bytes 1474576 | tf_op jit(solution)/shard_map/all_gather | solution.py:232
  545.4 3.9 bitcast_convert_fusion
  549.6 4.8 fusion.234
  563.4 13.5 %reduce-scatter.13.cloned.1.call-done = bf16[240,768]{1,0:T(8,128)(2,1)} async-done(((bf16[960,768]{1,0:T(8,128)(2,1)}), bf16[240,768]{1,0:T(8,128)(2,1)}) %reduce-scatter.13.cloned.1.call-update) | async-done | bytes 368656 | tf_op jit(solution)/shard_map/reduce_scatter | solution.py:269
  578.4 23.1 %all-reduce.3 = (f32[2,192]{1,0:T(2,128)}, f32[768]{0:T(1024)}) all-reduce(f32[2,192]{1,0:T(2,128)S(1)} %pad_maximum_fusion.7, f32[768]{0:T(1024)S(1)} %get-tuple-element.38), channel_id=1, replica_groups=mesh['dp'=8,'mp'=4] {'dp'}, use_global_device_ids=true, to_apply=%region_46.47 | all-reduce | flops 1152 | bytes 9216 | tf_op jit(solution)/shard_map/psum | solution.py:278
  601.5 41.9 %all-reduce.2 = (f32[]{:T(128)}, f32[6,768]{1,0:T(8,128)S(1)}) all-reduce(f32[]{:T(128)S(6)} %sub.157, f32[6,768]{1,0:T(8,128)S(1)} %stack.59), channel_id=1, replica_groups=mesh['dp'=8,'mp'=4] {'dp','mp'}, use_global_device_ids=true, to_apply=%region_30.31 | all-reduce | flops 4609 | bytes 36872 | tf_op jit(solution)/shard_map/psum | solution.py:193
  646.8 168.1 %all-reduce.7.cloned.1.call-done = (f32[3,768,192]{1,2,0:T(8,128)}, f32[192,768]{1,0:T(8,128)}, f32[768,768]{1,0:T(8,128)}, f32[768,768]{1,0:T(8,128)}) async-done(((f32[3,768,192]{1,2,0:T(8,128)}, f32[192,768]{1,0:T(8,128)}, f32[768,768]{1,0:T(8,128)}, f32[768,768]{1,0:T(8,128)}), (f32[3,768,192]{1,2,0:T(8,128)}, f32[192,768]{1,0:T(8,128)}, f32[768,768]{1,0:T(8,128)}, ...) | async-done | bytes 7077904 | tf_op jit(solution)/shard_map/psum | solution.py:278
  (302 shorter events, 129.2 us)
Async XLA Ops:
  7.2 226.8 %copy-start = (bf16[768,768]{1,0:T(8,128)(2,1)S(1)}, bf16[768,768]{1,0:T(8,128)(2,1)}, u32[]{:S(2)}) copy-start(bf16[768,768]{1,0:T(8,128)(2,1)} %param.32) | copy-start | bytes 3538948
  7.2 27.9 %all-gather.18.cloned.1.call-start = ((), (), s32[]{:S(2)}) async-start(), calls=%async_computation.8 | async-start | bytes 1843200 | tf_op jit(solution)/shard_map/all_gather | solution.py:132
  10.5 71.6 %copy-start.43 = (f32[768]{0:T(1024)}, f32[768]{0:T(1024)S(1)}, u32[]{:S(2)}) copy-start(f32[768]{0:T(1024)S(1)} %get-tuple-element.82) | copy-start | bytes 9220
  13.1 66.5 %reduce-scatter.7.cloned.1.call-start = ((), (), s32[]{:S(2)}) async-start(), calls=%async_computation.9 | async-start | bytes 1843200 | tf_op jit(solution)/shard_map/reduce_scatter | solution.py:151
  52.1 59.9 %all-gather.10.cloned.1.call-start = ((), (), s32[]{:S(2)}) async-start(), calls=%async_computation.4 | async-start | bytes 4423680 | tf_op jit(solution)/shard_map/all_gather | solution.py:106
  52.9 26.8 %copy-start.1 = (bf16[240,768]{1,0:T(8,128)(2,1)S(1)}, bf16[240,768]{1,0:T(8,128)(2,1)}, u32[]{:S(2)}) copy-start(bf16[240,768]{1,0:T(8,128)(2,1)} %param.19) | copy-start | bytes 1105924
  52.9 94.1 %all-gather.12.cloned.1.call-start = ((), (), s32[]{:S(2)}) async-start(), calls=%async_computation.5 | async-start | bytes 1474560 | tf_op jit(solution)/shard_map/all_gather | solution.py:107
  53.4 126.2 %all-gather.14.cloned.1.call-start = ((), (), s32[]{:S(2)}) async-start(), calls=%async_computation.6 | async-start | bytes 5898240 | tf_op jit(solution)/shard_map/all_gather | solution.py:108
  54.0 154.6 %all-gather.16.cloned.1.call-start = ((), (), s32[]{:S(2)}) async-start(), calls=%async_computation.7 | async-start | bytes 5898240 | tf_op jit(solution)/shard_map/all_gather | solution.py:109
  54.6 179.4 %all-gather.20.cloned.1.call-start = ((), (), s32[]{:S(2)}) async-start(), calls=%async_computation.10 | async-start | bytes 1843200 | tf_op jit(solution)/shard_map/all_gather | solution.py:161
  57.9 26.2 %copy-start.38 = (f32[768]{0:T(1024)}, f32[768]{0:T(1024)S(1)}, u32[]{:S(2)}) copy-start(f32[768]{0:T(1024)S(1)} %get-tuple-element.25) | copy-start | bytes 9220
  80.8 35.6 %copy-start.49 = (f32[240]{0:T(256)}, f32[240]{0:T(256)S(1)}, u32[]{:S(2)}) copy-start(f32[240]{0:T(256)S(1)} %broadcast_multiply_fusion.8) | copy-start | bytes 2884
  82.1 34.4 %copy-start.54 = (f32[240]{0:T(256)}, f32[240]{0:T(256)S(1)}, u32[]{:S(2)}) copy-start(f32[240]{0:T(256)S(1)} %add_rsqrt_fusion.4) | copy-start | bytes 2884
  84.1 191.2 %reduce-scatter.9.cloned.1.call-start = ((), (), s32[]{:S(2)}) async-start(), calls=%async_computation.11 | async-start | bytes 1843200 | tf_op jit(solution)/shard_map/reduce_scatter | solution.py:169
  208.6 25.4 %copy-start.64 = (f32[768]{0:T(1024)S(1)}, f32[768]{0:T(1024)}, u32[]{:S(2)}) copy-start(f32[768]{0:T(1024)} %param.33) | copy-start | bytes 9220
  247.7 215.6 %all-gather.22.cloned.1.call-start = ((), (), s32[]{:S(2)}) async-start(), calls=%async_computation.12 | async-start | bytes 1843200 | tf_op jit(solution)/shard_map/all_gather | solution.py:215
  276.9 42.8 %copy-start.59 = (f32[15]{0:T(128)}, f32[15]{0:T(128)S(1)}, u32[]{:S(2)}) copy-start(f32[15]{0:T(128)S(1)} %add_rsqrt_fusion.6) | copy-start | bytes 184
  437.9 4.3 collective-permute-start
  439.2 3.0 collective-permute-start.1
  444.1 57.5 %copy-start.28 = (f32[15,768]{1,0:T(8,128)}, f32[15,768]{1,0:T(8,128)S(1)}, u32[]{:S(2)}) copy-start(f32[15,768]{1,0:T(8,128)S(1)} %subtract_multiply_fusion.1) | copy-start | bytes 138244
  445.0 55.1 %reduce-scatter.11.cloned.1.call-start = ((), (), s32[]{:S(2)}) async-start(), calls=%async_computation.13 | async-start | bytes 1843200 | tf_op jit(solution)/shard_map/reduce_scatter | solution.py:223
  470.1 30.0 %copy-start.44 = (f32[768]{0:T(1024)S(1)}, f32[768]{0:T(1024)}, u32[]{:S(2)}) copy-start(f32[768]{0:T(1024)} %copy-done.43) | copy-start | bytes 9220
  470.1 30.0 %copy-start.50 = (f32[240]{0:T(256)S(1)}, f32[240]{0:T(256)}, u32[]{:S(2)}) copy-start(f32[240]{0:T(256)} %copy-done.49) | copy-start | bytes 2884
  470.1 30.0 %copy-start.55 = (f32[240]{0:T(256)S(1)}, f32[240]{0:T(256)}, u32[]{:S(2)}) copy-start(f32[240]{0:T(256)} %copy-done.54) | copy-start | bytes 2884
  472.5 32.6 %copy-start.32 = (f32[60,3,16]{2,1,0:T(4,128)S(1)}, f32[60,3,16]{2,1,0:T(4,128)}, u32[]{:S(2)}) copy-start(f32[60,3,16]{2,1,0:T(4,128)} %copy-done.31) | copy-start | bytes 34564
  472.5 32.6 %copy-start.34 = (f32[60,3,16]{2,1,0:T(4,128)S(1)}, f32[60,3,16]{2,1,0:T(4,128)}, u32[]{:S(2)}) copy-start(f32[60,3,16]{2,1,0:T(4,128)} %copy-done.33) | copy-start | bytes 34564
  472.6 51.4 %all-gather.24.cloned.1.call-start = ((), (), s32[]{:S(2)}) async-start(), calls=%async_computation.14 | async-start | bytes 1843200 | tf_op jit(solution)/shard_map/all_gather | solution.py:232
  503.9 25.1 %copy-start.4 = (f32[60,3,16,16]{2,3,1,0:T(8,128)S(1)}, f32[60,3,16,16]{2,3,1,0:T(8,128)}, u32[]{:S(2)}) copy-start(f32[60,3,16,16]{2,3,1,0:T(8,128)} %copy-done.3) | copy-start | bytes 552964
  504.7 72.2 %reduce-scatter.13.cloned.1.call-start = ((), (), s32[]{:S(2)}) async-start(), calls=%async_computation.15 | async-start | bytes 1843200 | tf_op jit(solution)/shard_map/reduce_scatter | solution.py:269
  549.4 265.5 %all-reduce.7.cloned.1.call-start = ((), (), s32[]{:S(2)}) async-start(), calls=%async_computation.16 | async-start | bytes 14155776 | tf_op jit(solution)/shard_map/psum | solution.py:278
  561.0 15.9 %copy-start.53 = (f32[240]{0:T(256)S(1)}, f32[240]{0:T(256)}, u32[]{:S(2)}) copy-start(f32[240]{0:T(256)} %copy-done.52) | copy-start | bytes 2884
  561.0 83.7 %copy-start.7 = (f32[240,768]{1,0:T(8,128)S(1)}, f32[240,768]{1,0:T(8,128)}, u32[]{:S(2)}) copy-start(f32[240,768]{1,0:T(8,128)} %copy-done.6) | copy-start | bytes 2211844
  (51 other events, 190.8 us)
Sparse Core Ops, SparseCore 0:
  13.2 21.7 all-gather.17
  52.2 27.3 reduce-scatter.6
  81.2 30.7 all-gather.9
  113.4 17.4 all-gather.11
  132.3 37.4 all-gather.13
  171.2 37.4 all-gather.15
  210.8 19.0 all-gather.19
  247.9 27.3 reduce-scatter.8
  445.1 18.2 all-gather.21
  472.7 27.3 reduce-scatter.10
  504.8 19.0 all-gather.23
  549.5 27.3 reduce-scatter.12
  581.9 232.9 all-reduce.6
where the time goes:
time: 839 us; the launch traced here: 829 us
  waiting for transfers between devices  347 us (41%)
  blocking collectives  222 us (26%)
  matrix products  125 us (15%)
  local copies, waits for them, and re-layouts  74.8 us (9%)
  other arithmetic  38.1 us (5%)
  between operations  18.9 us (2%)
    psum x1, waiting for transfers between devices, local(): lax.psum((grad_qkv, grad_qv_bias, grad_out, grad_fc1, grad_fc1_bias, grad...  168 us
    psum x2, blocking collectives, local(): summed, scalar = lax.psum((partial_value, own_term), ('dp', 'mp'))  78.7 us
    unnamed x1, blocking collectives  77.1 us
    dot_general x2, matrix products, image_tower(): result = middle + jnp.dot(active, w_fc2, preferred_element_type=jnp.float32)  45.9 us
    all_gather x1, blocking collectives, local(): arrived = lax.all_gather(captions16, ('dp', 'mp'), axis=0, tiled=True)  42.7 us
    all_gather x1, waiting for transfers between devices, local(): lax.all_gather(img_fc2, 'mp', axis=0, tiled=True)  29 us
    all_gather x1, waiting for transfers between devices, local(): lax.all_gather(img_qkv, 'mp', axis=2, tiled=True)  27.8 us
    reduce_scatter x1, waiting for transfers between devices, local(): lax.psum_scatter(jnp.einsum('gf,df->gd', grad_hidden16, txt_fc1, preferre...  27.5 us
  transfers between devices with their start and end apart: 15, of which 11 were waited for; matrix products, arithmetic and copies ran while one was open for 18% of the time, Pallas kernels for 0%

commit v1 on v0

--- a/solution.py
+++ b/solution.py
@@ -12,6 +12,18 @@
 SCALE = 40.0
 LOSS_SCALE = 16.0
 MASKED = -1e30
+
+
+def collect(x, axis, dim):
+    ways, here, lap = (lax.axis_size(axis), lax.axis_index(axis), x.shape[dim])
+    line, have = (x, 1)
+    while have < ways:
+        line = jnp.concatenate(
+            [line, lax.ppermute(line, axis, [(d, (d - have) % ways) for d in range(ways)])],
+            axis=dim,
+        )
+        have = 2 * have
+    return jnp.roll(line, here * lap, axis=dim)
 
 
 def layer_stats(values):
@@ -106,7 +118,7 @@
         lax.all_gather(img_qkv, "mp", axis=2, tiled=True),
         lax.all_gather(img_out, "mp", axis=0, tiled=True),
         lax.all_gather(img_fc1, "mp", axis=1, tiled=True),
-        lax.all_gather(img_fc2, "mp", axis=0, tiled=True),
+        collect(img_fc2, "mp", 0),
     )
     low_count = image_low.shape[0] // P_LOW
     high_count = image_high.shape[0] // P_HIGH

time: 839 us -> 861 us (1.026)
  local copies, waits for them, and re-layouts: 74.8 us -> 88.6 us
    ppermute x0 -> x2, waiting for transfers between devices: none -> 78.6 us  [collect(): lax.ppermute(line, axis, [(d, (d - have) % ways) for d in range(ways)])]
    all_gather x1 -> x0, waiting for transfers between devices: 29 us -> none  [local(): lax.all_gather(img_fc2, 'mp', axis=0, tiled=True)]
    all_gather x1, waiting for transfers between devices: 27.8 us -> 0.02 us  [local(): lax.all_gather(img_qkv, 'mp', axis=2, tiled=True)]
    reduce_scatter x1, waiting for transfers between devices: 20.6 us -> 0.01 us  [local(): lax.psum_scatter(jnp.dot(context, txt_out, preferred_element_type=jnp.flo...]
    unnamed x143 -> x162, local copies, waits for them, and re-layouts: 13.4 us -> 21.6 us
  transfers between devices with their start and end apart: 15 -> 16, of which waited for: 11 -> 10; matrix products, arithmetic and copies ran while one was open for 18% -> 19% of each run, Pallas kernels for 0% -> 0%
where the time goes in v1:
time: 861 us; the launch traced here: 851 us
  waiting for transfers between devices  348 us (40%)
  blocking collectives  221 us (26%)
  matrix products  125 us (15%)
  local copies, waits for them, and re-layouts  88.6 us (10%)
  other arithmetic  42.7 us (5%)
  between operations  19.3 us (2%)
    psum x1, waiting for transfers between devices, local(): lax.psum((grad_qkv, grad_qv_bias, grad_out, grad_fc1, grad_fc1_bias, grad...  168 us
    ppermute x2, waiting for transfers between devices, collect(): lax.ppermute(line, axis, [(d, (d - have) % ways) for d in range(ways)])  78.6 us
    psum x2, blocking collectives, local(): summed, scalar = lax.psum((partial_value, own_term), ('dp', 'mp'))  78.5 us
    unnamed x1, blocking collectives  77.1 us
    dot_general x2, matrix products, image_tower(): result = middle + jnp.dot(active, w_fc2, preferred_element_type=jnp.float32)  46.4 us
    all_gather x1, blocking collectives, local(): arrived = lax.all_gather(captions16, ('dp', 'mp'), axis=0, tiled=True)  42.7 us
    reduce_scatter x1, waiting for transfers between devices, local(): lax.psum_scatter(jnp.einsum('gf,df->gd', grad_hidden16, txt_fc1, preferre...  27.5 us
    psum x1, blocking collectives, local(): lax.psum((grad_qkv, grad_qv_bias, grad_out, grad_fc1, grad_fc1_bias, grad...  23.1 us
  transfers between devices with their start and end apart: 16, of which 10 were waited for; matrix products, arithmetic and copies ran while one was open for 19% of the time, Pallas kernels for 0%

profile of v1, /device:TPU:0, one launch (start us, length us, event | category | flops | bytes accessed | tf_op | source)
XLA Modules:
  0.0 851.0 jit_solution(17163631146982911660)
XLA Ops:
  14.9 20.2 %all-gather.15.cloned.1.call-done = bf16[960,768]{1,0:T(8,128)(2,1)} async-done(((bf16[240,768]{1,0:T(8,128)(2,1)}), bf16[960,768]{1,0:T(8,128)(2,1)}) %all-gather.15.cloned.1.call-update) | async-done | bytes 1474576 | tf_op jit(solution)/shard_map/all_gather | solution.py:144
  43.9 3.2 fusion.258
  54.3 13.7 %collective-permute-done = bf16[768,768]{1,0:T(8,128)(2,1)S(1)} collective-permute-done((bf16[768,768]{1,0:T(8,128)(2,1)S(1)}, bf16[768,768]{1,0:T(8,128)(2,1)S(1)}, u32[]{:S(2)}, u32[]{:S(2)}) %collective-permute-start) | collective-permute-done | bytes 1179680 | tf_op jit(solution)/shard_map/ppermute | solution.py:22
  83.6 64.9 %collective-permute-done.1 = bf16[1536,768]{1,0:T(8,128)(2,1)} collective-permute-done((bf16[1536,768]{1,0:T(8,128)(2,1)}, bf16[1536,768]{1,0:T(8,128)(2,1)}, u32[]{:S(2)}, u32[]{:S(2)}) %collective-permute-start.1) | collective-permute-done | bytes 2359328 | tf_op jit(solution)/shard_map/ppermute | solution.py:22
  148.5 3.2 constant_dynamic-update-slice_fusion.3
  153.9 3.3 constant_dynamic-update-slice_fusion
  161.9 4.7 convert_bitcast_fusion
  168.0 4.5 squeeze.30
  172.5 4.1 squeeze.31
  176.6 3.7 fusion.76
  180.3 3.2 fusion.266
  186.3 4.3 convert_bitcast_fusion.1
  192.4 4.2 reshape.220
  206.5 3.3 reshape.237
  212.2 3.8 fusion.264
  218.3 4.1 fusion.99
  229.4 25.6 %fusion.88 = f32[600,768]{1,0:T(8,128)S(1)} fusion(f32[600,768]{1,0:T(8,128)} %copy-done.25, bf16[6144,768]{1,0:T(8,128)(2,1)} %constant_dynamic-update-slice_fusion, s32[]{:T(128)S(6)} %select_n.25, bf16[768,3072]{1,0:T(8,128)(2,1)} %all-gather.13.cloned.1.call-done, f32[768]{0:T(1024)S(1)} %copy-done.63, f32[600]{0:T(1024)S(1)} %add_rsqrt_fusion, ...), kind=kOutput, calls=%fused_computation.132 | convolution fusion | flops 5784422400 | bytes 14974660 | tf_op jit(solution)/shard_map/dot_general | solution.py:89
  255.0 10.1 %multiply_convert_fusion = (bf16[960,768]{1,0:T(8,128)(2,1)S(1)}, f32[960,768]{1,0:T(8,128)}, f32[960,768]{1,0:T(8,128)}) fusion(f32[768]{0:T(1024)S(1)} %copy-done.71, bf16[960,768]{1,0:T(8,128)(2,1)} %all-gather.17.cloned.1.call-done, bf16[768,768]{1,0:T(8,128)(2,1)S(1)} %copy-done), kind=kOutput, calls=%fused_computation.57 | convolution fusion | flops 1181122560 | bytes 10030080 | tf_op jit(solution)/shard_map/dot_general | solution.py:174
  268.9 20.8 %fusion.102 = f32[435,768]{1,0:T(8,128)} fusion(f32[435,768]{1,0:T(8,128)} %copy-done.27, bf16[6144,768]{1,0:T(8,128)(2,1)} %constant_dynamic-update-slice_fusion, s32[]{:T(128)S(6)} %select_n.25, bf16[768,3072]{1,0:T(8,128)(2,1)} %all-gather.13.cloned.1.call-done, f32[768]{0:T(1024)S(1)} %copy-done.63, f32[435]{0:T(512)S(1)} %add_rsqrt_fusion.2, ...), kind=kOutput, calls=%fused_computation.152 | convolution fusion | flops 4193706240 | bytes 13483420 | tf_op jit(solution)/shard_map/dot_general | solution.py:89
  298.4 42.7 %all-gather = bf16[32,15,768]{2,1,0:T(8,128)(2,1)S(1)} all-gather(bf16[1,15,768]{2,1,0:T(8,128)(2,1)S(1)} %fusion.174), channel_id=1, replica_groups=mesh['dp'=8,'mp'=4] {'dp','mp'}, dimensions={0}, use_global_device_ids=true | all-gather | bytes 760320 | tf_op jit(solution)/shard_map/all_gather | solution.py:197
  342.9 36.8 %psum.64 = f32[480]{0:T(512)S(1)} all-reduce(f32[480]{0:T(512)S(1)} %get-tuple-element.19), channel_id=1, replica_groups=mesh['dp'=8,'mp'=4] {'dp','mp'}, use_global_device_ids=true, to_apply=%region_32.33 | all-reduce | flops 480 | bytes 3840 | tf_op jit(solution)/shard_map/psum | solution.py:205
  382.1 77.1 %fusion = f32[16,768]{1,0:T(8,128)S(1)} fusion(f32[480,768]{1,0:T(8,128)S(1)} %convolution_multiply_fusion), kind=kCustom, calls=%all-reduce-scatter | all-reduce-scatter fusion | flops 393217 | bytes 1523712
  466.4 18.3 %all-gather.19.cloned.1.call-done = bf16[960,768]{1,0:T(8,128)(2,1)} async-done(((bf16[240,768]{1,0:T(8,128)(2,1)}), bf16[960,768]{1,0:T(8,128)(2,1)}) %all-gather.19.cloned.1.call-update) | async-done | bytes 1474576 | tf_op jit(solution)/shard_map/all_gather | solution.py:227
  484.8 5.6 convert_reduce_fusion
  494.0 27.5 %reduce-scatter.11.cloned.1.call-done = bf16[240,768]{1,0:T(8,128)(2,1)} async-done(((bf16[960,768]{1,0:T(8,128)(2,1)}), bf16[240,768]{1,0:T(8,128)(2,1)}) %reduce-scatter.11.cloned.1.call-update) | async-done | bytes 368656 | tf_op jit(solution)/shard_map/reduce_scatter | solution.py:235
  527.3 18.1 %all-gather.21.cloned.1.call-done = bf16[960,768]{1,0:T(8,128)(2,1)} async-done(((bf16[240,768]{1,0:T(8,128)(2,1)}), bf16[960,768]{1,0:T(8,128)(2,1)}) %all-gather.21.cloned.1.call-update) | async-done | bytes 1474576 | tf_op jit(solution)/shard_map/all_gather | solution.py:244
  566.9 3.9 bitcast_convert_fusion
  571.1 4.8 fusion.271
  584.9 13.6 %reduce-scatter.13.cloned.1.call-done = bf16[240,768]{1,0:T(8,128)(2,1)} async-done(((bf16[960,768]{1,0:T(8,128)(2,1)}), bf16[240,768]{1,0:T(8,128)(2,1)}) %reduce-scatter.13.cloned.1.call-update) | async-done | bytes 368656 | tf_op jit(solution)/shard_map/reduce_scatter | solution.py:281
  600.0 23.1 %all-reduce.3 = (f32[2,192]{1,0:T(2,128)}, f32[768]{0:T(1024)}) all-reduce(f32[2,192]{1,0:T(2,128)S(1)} %pad_maximum_fusion.8, f32[768]{0:T(1024)S(1)} %get-tuple-element.38), channel_id=1, replica_groups=mesh['dp'=8,'mp'=4] {'dp'}, use_global_device_ids=true, to_apply=%region_46.47 | all-reduce | flops 1152 | bytes 9216 | tf_op jit(solution)/shard_map/psum | solution.py:290
  623.1 41.7 %all-reduce.2 = (f32[]{:T(128)}, f32[6,768]{1,0:T(8,128)S(1)}) all-reduce(f32[]{:T(128)S(6)} %sub.162, f32[6,768]{1,0:T(8,128)S(1)} %stack.59), channel_id=1, replica_groups=mesh['dp'=8,'mp'=4] {'dp','mp'}, use_global_device_ids=true, to_apply=%region_30.31 | all-reduce | flops 4609 | bytes 36872 | tf_op jit(solution)/shard_map/psum | solution.py:205
  668.2 168.0 %all-reduce.7.cloned.1.call-done = (f32[3,768,192]{1,2,0:T(8,128)}, f32[192,768]{1,0:T(8,128)}, f32[768,768]{1,0:T(8,128)}, f32[768,768]{1,0:T(8,128)}) async-done(((f32[3,768,192]{1,2,0:T(8,128)}, f32[192,768]{1,0:T(8,128)}, f32[768,768]{1,0:T(8,128)}, f32[768,768]{1,0:T(8,128)}), (f32[3,768,192]{1,2,0:T(8,128)}, f32[192,768]{1,0:T(8,128)}, f32[768,768]{1,0:T(8,128)}, ...) | async-done | bytes 7077904 | tf_op jit(solution)/shard_map/psum | solution.py:290
  (324 shorter events, 145.6 us)
Async XLA Ops:
  7.2 247.8 %copy-start = (bf16[768,768]{1,0:T(8,128)(2,1)S(1)}, bf16[768,768]{1,0:T(8,128)(2,1)}, u32[]{:S(2)}) copy-start(bf16[768,768]{1,0:T(8,128)(2,1)} %param.32) | copy-start | bytes 3538948
  7.2 27.9 %all-gather.15.cloned.1.call-start = ((), (), s32[]{:S(2)}) async-start(), calls=%async_computation.7 | async-start | bytes 1843200 | tf_op jit(solution)/shard_map/all_gather | solution.py:144
  10.5 149.2 %copy-start.45 = (f32[768]{0:T(1024)}, f32[768]{0:T(1024)S(1)}, u32[]{:S(2)}) copy-start(f32[768]{0:T(1024)S(1)} %get-tuple-element.82) | copy-start | bytes 9220
  13.1 144.2 %reduce-scatter.7.cloned.1.call-start = ((), (), s32[]{:S(2)}) async-start(), calls=%async_computation.8 | async-start | bytes 1843200 | tf_op jit(solution)/shard_map/reduce_scatter | solution.py:163
  52.1 109.7 %all-gather.9.cloned.1.call-start = ((), (), s32[]{:S(2)}) async-start(), calls=%async_computation.4 | async-start | bytes 4423680 | tf_op jit(solution)/shard_map/all_gather | solution.py:118
  52.9 143.8 %all-gather.11.cloned.1.call-start = ((), (), s32[]{:S(2)}) async-start(), calls=%async_computation.5 | async-start | bytes 1474560 | tf_op jit(solution)/shard_map/all_gather | solution.py:119
  53.4 175.9 %all-gather.13.cloned.1.call-start = ((), (), s32[]{:S(2)}) async-start(), calls=%async_computation.6 | async-start | bytes 5898240 | tf_op jit(solution)/shard_map/all_gather | solution.py:120
  54.0 200.9 %all-gather.17.cloned.1.call-start = ((), (), s32[]{:S(2)}) async-start(), calls=%async_computation.9 | async-start | bytes 1843200 | tf_op jit(solution)/shard_map/all_gather | solution.py:173
  54.1 13.9 %collective-permute-start = (bf16[768,768]{1,0:T(8,128)(2,1)S(1)}, bf16[768,768]{1,0:T(8,128)(2,1)S(1)}, u32[]{:S(2)}, u32[]{:S(2)}) collective-permute-start(bf16[768,768]{1,0:T(8,128)(2,1)S(1)} %copy-done.6), channel_id=1, source_target_pairs={{0,3},{1,0},{2,1},{3,2},{4,7},{5,4},{6,5},{7,6},{8,11},{9,8},{10,9... | collective-permute-start | bytes 3538952 | tf_op jit(solution)/shard_map/ppermute | solution.py:22
  69.6 78.9 %collective-permute-start.1 = (bf16[1536,768]{1,0:T(8,128)(2,1)}, bf16[1536,768]{1,0:T(8,128)(2,1)}, u32[]{:S(2)}, u32[]{:S(2)}) collective-permute-start(bf16[1536,768]{1,0:T(8,128)(2,1)} %pad_maximum_fusion), channel_id=1, source_target_pairs={{0,2},{1,3},{2,0},{3,1},{4,6},{5,7},{6,4},{7,5},{8,10},{9,11},{10,... | collective-permute-start | bytes 7077896 | tf_op jit(solution)/shard_map/ppermute | solution.py:22
  77.4 82.4 %copy-start.40 = (f32[768]{0:T(1024)}, f32[768]{0:T(1024)S(1)}, u32[]{:S(2)}) copy-start(f32[768]{0:T(1024)S(1)} %get-tuple-element.25) | copy-start | bytes 9220
  80.9 70.8 %copy-start.58 = (f32[600]{0:T(1024)}, f32[600]{0:T(1024)S(1)}, u32[]{:S(2)}) copy-start(f32[600]{0:T(1024)S(1)} %broadcast_multiply_fusion.1) | copy-start | bytes 7204
  161.7 135.0 %reduce-scatter.9.cloned.1.call-start = ((), (), s32[]{:S(2)}) async-start(), calls=%async_computation.10 | async-start | bytes 1843200 | tf_op jit(solution)/shard_map/reduce_scatter | solution.py:181
  229.4 25.6 %copy-start.71 = (f32[768]{0:T(1024)S(1)}, f32[768]{0:T(1024)}, u32[]{:S(2)}) copy-start(f32[768]{0:T(1024)} %param.33) | copy-start | bytes 9220
  268.7 216.1 %all-gather.19.cloned.1.call-start = ((), (), s32[]{:S(2)}) async-start(), calls=%async_computation.11 | async-start | bytes 1843200 | tf_op jit(solution)/shard_map/all_gather | solution.py:227
  298.3 42.8 %copy-start.62 = (f32[15]{0:T(128)}, f32[15]{0:T(128)S(1)}, u32[]{:S(2)}) copy-start(f32[15]{0:T(128)S(1)} %add_rsqrt_fusion.6) | copy-start | bytes 184
  459.3 4.3 collective-permute-start.2
  460.6 3.0 collective-permute-start.3
  465.5 57.5 %copy-start.30 = (f32[15,768]{1,0:T(8,128)}, f32[15,768]{1,0:T(8,128)S(1)}, u32[]{:S(2)}) copy-start(f32[15,768]{1,0:T(8,128)S(1)} %subtract_multiply_fusion.1) | copy-start | bytes 138244
  466.4 55.2 %reduce-scatter.11.cloned.1.call-start = ((), (), s32[]{:S(2)}) async-start(), calls=%async_computation.12 | async-start | bytes 1843200 | tf_op jit(solution)/shard_map/reduce_scatter | solution.py:235
  491.5 30.1 %copy-start.46 = (f32[768]{0:T(1024)S(1)}, f32[768]{0:T(1024)}, u32[]{:S(2)}) copy-start(f32[768]{0:T(1024)} %copy-done.45) | copy-start | bytes 9220
  491.5 30.1 %copy-start.51 = (f32[240]{0:T(256)S(1)}, f32[240]{0:T(256)}, u32[]{:S(2)}) copy-start(f32[240]{0:T(256)} %copy-done.50) | copy-start | bytes 2884
  491.5 30.1 %copy-start.56 = (f32[240]{0:T(256)S(1)}, f32[240]{0:T(256)}, u32[]{:S(2)}) copy-start(f32[240]{0:T(256)} %copy-done.55) | copy-start | bytes 2884
  493.9 32.7 %copy-start.34 = (f32[60,3,16]{2,1,0:T(4,128)S(1)}, f32[60,3,16]{2,1,0:T(4,128)}, u32[]{:S(2)}) copy-start(f32[60,3,16]{2,1,0:T(4,128)} %copy-done.33) | copy-start | bytes 34564
  493.9 32.7 %copy-start.36 = (f32[60,3,16]{2,1,0:T(4,128)S(1)}, f32[60,3,16]{2,1,0:T(4,128)}, u32[]{:S(2)}) copy-start(f32[60,3,16]{2,1,0:T(4,128)} %copy-done.35) | copy-start | bytes 34564
  494.0 51.5 %all-gather.21.cloned.1.call-start = ((), (), s32[]{:S(2)}) async-start(), calls=%async_computation.13 | async-start | bytes 1843200 | tf_op jit(solution)/shard_map/all_gather | solution.py:244
  525.4 25.1 %copy-start.4 = (f32[60,3,16,16]{2,3,1,0:T(8,128)S(1)}, f32[60,3,16,16]{2,3,1,0:T(8,128)}, u32[]{:S(2)}) copy-start(f32[60,3,16,16]{2,3,1,0:T(8,128)} %copy-done.3) | copy-start | bytes 552964
  526.2 72.3 %reduce-scatter.13.cloned.1.call-start = ((), (), s32[]{:S(2)}) async-start(), calls=%async_computation.14 | async-start | bytes 1843200 | tf_op jit(solution)/shard_map/reduce_scatter | solution.py:281
  570.9 265.4 %all-reduce.7.cloned.1.call-start = ((), (), s32[]{:S(2)}) async-start(), calls=%async_computation.15 | async-start | bytes 14155776 | tf_op jit(solution)/shard_map/psum | solution.py:290
  582.5 16.0 %copy-start.49 = (f32[240]{0:T(256)S(1)}, f32[240]{0:T(256)}, u32[]{:S(2)}) copy-start(f32[240]{0:T(256)} %copy-done.48) | copy-start | bytes 2884
  582.5 16.0 %copy-start.54 = (f32[240]{0:T(256)S(1)}, f32[240]{0:T(256)}, u32[]{:S(2)}) copy-start(f32[240]{0:T(256)} %copy-done.53) | copy-start | bytes 2884
  582.5 83.6 %copy-start.8 = (f32[240,768]{1,0:T(8,128)S(1)}, f32[240,768]{1,0:T(8,128)}, u32[]{:S(2)}) copy-start(f32[240,768]{1,0:T(8,128)} %copy-done.7) | copy-start | bytes 2211844
  (59 other events, 228.9 us)
Sparse Core Ops, SparseCore 0:
  13.2 21.7 all-gather.14
  52.2 32.4 reduce-scatter.6
  86.3 49.6 all-gather.8
  137.4 18.4 all-gather.10
  157.2 37.4 all-gather.12
  196.7 19.0 all-gather.16
  268.8 27.8 reduce-scatter.8
  466.5 18.2 all-gather.18
  494.1 27.3 reduce-scatter.10
  526.3 19.0 all-gather.20
  571.0 27.4 reduce-scatter.12
  603.3 232.9 all-reduce.6
